TPU v7x, 32 devices: a whole 2x2x4 slice. The times are simulated.
32 devices in a mesh: groups: 2 (over x), seq: 8 (over z, y), mp: 2 (over core).
Axes of the slice: x: 2, y: 2, z: 4, core: 2. Of those that a mesh axis runs over, the one named last changes fastest.
Arguments:
- latent_cache: bfloat16 [2048, 64, 512], P(('groups', 'seq')), parts along dimension 0, may hold values from -6 to 6
- rope_cache: bfloat16 [2048, 4096], P(('groups', 'seq')), parts along dimension 0, may hold values from -6 to 6
- q_nope: bfloat16 [16, 128, 128], P('groups', 'mp'), parts along dimension 0, may hold values from -12 to 12
- q_rope: bfloat16 [16, 128, 64], P('groups', 'mp'), parts along dimension 0, may hold values from -2000 to 2000
- w_uk: bfloat16 [128, 128, 512], P('mp', None, 'seq'), may hold values from -0.5 to 0.5
- value_up_weight: bfloat16 [128, 512, 128], P('mp', 'seq'), may hold values from -0.25 to 0.25
- w_out: bfloat16 [16384, 7168], P('mp', 'seq'), may hold values from -0.046875 to 0.046875
- page_table: int32 [16, 256], P('groups'), parts along dimension 0, may hold values from 0 to 1023, as said below
- lengths: int32 [16], P('groups'), parts along dimension 0, may hold values from 2048 to 16384, as said below
Outputs:
- output: bfloat16 [16, 7168], P('groups', ('seq', 'mp')), parts along dimension 0
There are 2 independent parts, one for each index of `groups`. A program takes and returns all parts, laid end to end along the dimension named above; an argument that names none is the same for every part. Nothing has to cross between parts.
Inputs may be any that keep to these rules, and one draw needn't show every extreme that they name: `lengths`: every sequence has one eighth of 16384 tokens or more; the longest has exactly 16384. page_table[b,p] for p < ceil(lengths[b] / 64) is the global slot (shard index times 128 plus local slot) holding that page; these live entries are all distinct; the other entries are 0 and unused.
All inputs are finite; a program needn't handle non-finite values.
Results may differ from a plain program's by a relative error of at most 0.012.
Values may be sent and summed in bfloat16 or wider, within the bound.
A program may use at most 128 MiB of HBM per device.

v0:
```python
import jax
import jax.numpy as jnp
from jax import lax
from jax.sharding import PartitionSpec as P

NEG = -1e30


def local(
    latent_cache, rope_cache, q_nope, q_rope, w_uk, value_up_weight, w_out, page_table, lengths
):
    peak_score = lax.Precision.HIGHEST
    slots_dev, page_len, latent_width = latent_cache.shape
    rope_width = q_rope.shape[2]
    seq_count, heads = (q_nope.shape[0], q_nope.shape[1])
    score_scale = (q_nope.shape[2] + rope_width) ** (-0.5)
    q_part = jnp.einsum("bhn,hnk->bhk", q_nope, w_uk, preferred_element_type=jnp.float32).astype(
        jnp.bfloat16
    )
    q_latent = lax.all_gather(q_part, "seq", axis=2, tiled=True)
    first_slot = lax.axis_index("seq") * slots_dev
    page_count = (lengths + page_len - 1) // page_len
    logical = jnp.arange(page_table.shape[1], dtype=jnp.int32)
    live_page = logical[None, :] < page_count[:, None]
    tokens_in = jnp.clip(lengths[:, None] - page_len * logical[None, :], 0, page_len)
    local_ids = jnp.arange(slots_dev, dtype=jnp.int32)
    hits = ((page_table - first_slot)[:, :, None] == local_ids[None, None, :]) & live_page[
        :, :, None
    ]
    owner_mask = jnp.any(hits, axis=1)
    slot_fill = jnp.sum(jnp.where(hits, tokens_in[:, :, None], 0), axis=(0, 1))
    owner_half = owner_mask.astype(jnp.bfloat16)

    def update(run_state, index):
        run_max, run_sum, run_out = run_state
        start = index * 8
        latent_block = lax.dynamic_slice_in_dim(latent_cache, start, 8, 0)
        rope_block = lax.dynamic_slice_in_dim(rope_cache, start, 8, 0).reshape(
            8, page_len, rope_width
        )
        owner_block = lax.dynamic_slice_in_dim(owner_half, start, 8, 1)
        fill_block = lax.dynamic_slice_in_dim(slot_fill, start, 8, 0)
        pick_latent = jnp.einsum(
            "bs,bhk->shk", owner_block, q_latent, preferred_element_type=jnp.float32
        ).astype(jnp.bfloat16)
        pick_rope = jnp.einsum(
            "bs,bhr->shr", owner_block, q_rope, preferred_element_type=jnp.float32
        ).astype(jnp.bfloat16)
        scores = (
            jnp.einsum(
                "shk,stk->sht", pick_latent, latent_block, preferred_element_type=jnp.float32
            )
            + jnp.einsum("shr,str->sht", pick_rope, rope_block, preferred_element_type=jnp.float32)
        ) * score_scale
        live_token = (
            jnp.arange(page_len, dtype=jnp.int32)[None, None, :] < fill_block[:, None, None]
        )
        slot_max = jnp.max(jnp.where(live_token, scores, NEG), axis=2)
        exponent = jnp.where(live_token, jnp.exp(scores - slot_max[:, :, None]), 0.0)
        slot_sum = jnp.sum(exponent, axis=2)
        slot_out = jnp.einsum(
            "sht,stk->shk",
            exponent.astype(jnp.bfloat16),
            latent_block,
            preferred_element_type=jnp.float32,
        )
        owned = owner_block > 0
        candidate = jnp.where(owned[:, :, None], slot_max[None, :, :], NEG)
        new_max = jnp.maximum(run_max, jnp.max(candidate, axis=1))
        carry_scale = jnp.exp(run_max - new_max)
        factor = jnp.where(owned[:, :, None], jnp.exp(candidate - new_max[:, None, :]), 0.0)
        run_sum = run_sum * carry_scale + jnp.einsum(
            "bsh,sh->bh", factor, slot_sum, precision=peak_score
        )
        run_out = run_out * carry_scale[:, :, None] + jnp.einsum(
            "bsh,shk->bhk", factor, slot_out, precision=peak_score
        )
        return (new_max, run_sum, run_out)

    def visit(index, run_state):
        return update(run_state, index)

    initial = (
        jnp.full((seq_count, heads), NEG, jnp.float32),
        jnp.zeros((seq_count, heads), jnp.float32),
        jnp.zeros((seq_count, heads, latent_width), jnp.float32),
    )
    run_max, run_sum, run_out = lax.fori_loop(0, slots_dev // 8, visit, initial)
    share_width = value_up_weight.shape[1]
    shards = lax.axis_size("seq")
    spread_max = jnp.broadcast_to(run_max[:, :, None], (seq_count, heads, shards))
    spread_sum = jnp.broadcast_to(run_sum[:, :, None], (seq_count, heads, shards))
    peers_max, peers_sum, peers_out = (
        lax.all_to_all(spread_max, "seq", split_axis=2, concat_axis=2, tiled=True),
        lax.all_to_all(spread_sum, "seq", split_axis=2, concat_axis=2, tiled=True),
        lax.all_to_all(run_out, "seq", split_axis=2, concat_axis=2, tiled=True),
    )
    top = jnp.max(peers_max, axis=2)
    rescale = jnp.exp(peers_max - top[:, :, None])
    totals = jnp.sum(peers_sum * rescale, axis=2)
    grouped = peers_out.reshape(seq_count, heads, shards, share_width)
    shared_latent = jnp.sum(grouped * rescale[:, :, :, None], axis=2)
    local_portion = (shared_latent / totals[:, :, None]).astype(jnp.bfloat16)
    value_slice = jnp.einsum(
        "gre,req->grq", local_portion, value_up_weight, preferred_element_type=jnp.float32
    )
    value_rows = lax.psum(value_slice, "seq").astype(jnp.bfloat16)
    flat_values = value_rows.reshape(seq_count, heads * value_rows.shape[2])
    partial_out = jnp.dot(flat_values, w_out, preferred_element_type=jnp.float32)
    return lax.psum_scatter(partial_out, "mp", scatter_dimension=1, tiled=True).astype(jnp.bfloat16)


def solution(mesh):
    return jax.shard_map(
        local,
        mesh=mesh,
        in_specs=(
            P(("groups", "seq"), None, None),
            P(("groups", "seq"), None),
            P("groups", "mp", None),
            P("groups", "mp", None),
            P("mp", None, "seq"),
            P("mp", "seq", None),
            P("mp", "seq"),
            P("groups", None),
            P("groups"),
        ),
        out_specs=P("groups", ("seq", "mp")),
        check_vma=False,
    )
```

profile of v0, /device:TPU:0, one launch (start us, length us, event | category | flops | bytes accessed | tf_op | source)
XLA Modules:
  0.0 317.1 jit_solution(13368818275387407663)
XLA Ops:
  10.1 1.9 fusion.40
  13.1 36.4 %all_gather.3 = bf16[8,64,512]{1,0,2:T(8,128)(2,1)} all-gather(bf16[8,64,64]{1,0,2:T(8,128)(2,1)S(1)} %copy.63), channel_id=1, replica_groups=mesh['groups'=2,'seq'=8,'mp'=2] {'seq'}, dimensions={2}, use_global_device_ids=true | all-gather | bytes 589824 | tf_op jit(solution)/shard_map/all_gather | solution.py:20
  49.6 2.3 copy.65
  51.9 129.9 %while.18 = (s32[]{:T(128)}, f32[8,64]{0,1:T(8,128)S(1)}, f32[8,64]{0,1:T(8,128)S(1)}, f32[8,64,512]{2,0,1:T(8,128)S(1)}, bf16[8,128]{1,0:T(8,128)(2,1)S(1)}, /*...) while((s32[]{:T(128)}, f32[8,64]{0,1:T(8,128)S(1)}, ...), condition=%wide.region_6.7_spmd.clone, body=%wide.region_2.6_spmd.clone.sunk | while | flops 102681152 | bytes 8056379 | solution.py:88
  56.7 1.5 fusion.90
  58.2 1.8 fusion.91
  64.8 1.5 fusion.90
  66.3 1.8 fusion.91
  72.9 1.5 fusion.90
  74.5 1.8 fusion.91
  81.0 1.5 fusion.90
  82.6 1.8 fusion.91
  89.2 1.5 fusion.90
  90.7 1.8 fusion.91
  97.3 1.5 fusion.90
  98.8 1.8 fusion.91
  105.4 1.5 fusion.90
  106.9 1.8 fusion.91
  113.5 1.5 fusion.90
  115.0 1.8 fusion.91
  123.2 1.8 fusion.91
  131.3 1.8 fusion.91
  137.9 1.5 fusion.90
  139.4 1.8 fusion.91
  146.0 1.5 fusion.90
  147.5 1.8 fusion.91
  155.6 1.8 fusion.91
  163.7 1.8 fusion.91
  170.3 1.5 fusion.90
  171.9 1.8 fusion.91
  178.5 1.5 fusion.90
  180.0 1.8 fusion.91
  182.5 5.3 %all-to-all-start.2 = ((f32[8,1,512]{2,1,0:T(1,128)}), f32[8,1,512]{2,1,0:T(1,128)S(1)}, u32[]{:S(2)}, u32[]{:S(2)}) async-start(f32[8,1,512]{2,1,0:T(1,128)} %reshape.112), calls=%async_computation.2 | async-start | bytes 32768 | tf_op jit(solution)/shard_map/all_to_all | solution.py:95
  188.6 5.8 %all-to-all-done.2 = f32[8,1,512]{2,1,0:T(1,128)S(1)} async-done(((f32[8,1,512]{2,1,0:T(1,128)}), f32[8,1,512]{2,1,0:T(1,128)S(1)}, u32[]{:S(2)}, u32[]{:S(2)}) %all-to-all-start.2) | async-done | bytes 16416 | tf_op jit(solution)/shard_map/all_to_all | solution.py:95
  194.4 3.3 %all-to-all-start.1 = ((f32[8,1,512]{2,1,0:T(1,128)}), f32[8,1,512]{2,1,0:T(1,128)S(1)}, u32[]{:S(2)}, u32[]{:S(2)}) async-start(f32[8,1,512]{2,1,0:T(1,128)} %reshape.110), calls=%async_computation.1 | async-start | bytes 32768 | tf_op jit(solution)/shard_map/all_to_all | solution.py:94
  197.8 2.3 copy.67
  200.1 3.4 %reshape.108 = f32[8,1,32768]{2,1,0:T(1,128)} reshape(f32[512,8,64]{2,1,0:T(8,128)} %bitcast.64) | data formatting | bytes 2097152
  204.4 5.0 %all-to-all-start = ((f32[8,1,32768]{2,1,0:T(1,128)}), f32[8,1,32768]{2,1,0:T(1,128)S(1)}, u32[]{:S(2)}, u32[]{:S(2)}) async-start(f32[8,1,32768]{2,1,0:T(1,128)} %reshape.108), calls=%async_computation | async-start | bytes 2097152 | tf_op jit(solution)/shard_map/all_to_all | solution.py:96
  211.9 16.0 %all-to-all-done = f32[8,1,32768]{2,1,0:T(1,128)S(1)} async-done(((f32[8,1,32768]{2,1,0:T(1,128)}), f32[8,1,32768]{2,1,0:T(1,128)S(1)}, u32[]{:S(2)}, u32[]{:S(2)}) %all-to-all-start) | async-done | bytes 1048608 | tf_op jit(solution)/shard_map/all_to_all | solution.py:96
  227.9 3.1 reduce
  231.0 2.2 reshape.109
  233.2 9.4 %copy.70 = f32[8,64,8,64]{0,1,3,2:T(8,128)} copy(f32[8,64,8,64]{1,0,3,2:T(8,128)} %bitcast.63) | data formatting | bytes 2097152 | tf_op jit(solution)/shard_map/reshape | solution.py:101
  242.6 9.7 %multiply_reduce_fusion = f32[8,64,64]{0,1,2:T(8,128)} fusion(f32[8,64,8,64]{0,1,3,2:T(8,128)} %copy.70, f32[8,64,8]{0,1,2:T(8,128)S(1)} %copy.69), kind=kLoop, calls=%fused_computation.53 | loop fusion | flops 491520 | bytes 1196032 | tf_op jit(solution)/shard_map/reduce_sum | solution.py:102
  252.3 2.7 copy.72
  255.5 38.2 %all-reduce.1 = bf16[8,64,128]{2,0,1:T(8,128)(2,1)S(1)} all-reduce(f32[8,64,128]{2,0,1:T(8,128)S(1)} %convolution_bitcast_fusion.2), channel_id=1, replica_groups=mesh['groups'=2,'seq'=8,'mp'=2] {'seq'}, use_global_device_ids=true, to_apply=%region_10.11 | all-reduce | flops 65536 | bytes 393216 | tf_op jit(solution)/shard_map/psum | solution.py:107
  293.8 9.8 %convolution_bitcast_fusion.1 = f32[896,8]{1,0:T(8,128)} fusion(bf16[8192,896]{1,0:T(8,128)(2,1)} %param.17, bf16[8,64,128]{2,0,1:T(8,128)(2,1)S(1)} %all-reduce.1), kind=kOutput, calls=%fused_computation.54 | convolution fusion | flops 117440512 | bytes 14839808
  303.6 5.1 %reduce-scatter.4.cloned.1.call-done = f32[448,8]{1,0:T(8,128)} async-done(((f32[896,8]{1,0:T(8,128)}), f32[448,8]{1,0:T(8,128)}) %reduce-scatter.4.cloned.1.call-update) | async-done | bytes 14352
  308.6 1.6 copy.78
  (357 shorter events, 91.8 us)
Async XLA Ops:
  6.5 248.6 %copy-start = (bf16[64,64,128]{2,1,0:T(8,128)(2,1)S(1)}, bf16[64,64,128]{2,1,0:T(8,128)(2,1)}, u32[]{:S(2)}) copy-start(bf16[64,64,128]{2,1,0:T(8,128)(2,1)} %param.16) | copy-start | bytes 3145732
  182.5 11.9 %all-to-all-start.2 = ((f32[8,1,512]{2,1,0:T(1,128)}), f32[8,1,512]{2,1,0:T(1,128)S(1)}, u32[]{:S(2)}, u32[]{:S(2)}) async-start(f32[8,1,512]{2,1,0:T(1,128)} %reshape.112), calls=%async_computation.2 | async-start | bytes 32768 | tf_op jit(solution)/shard_map/all_to_all | solution.py:95
  194.4 9.9 %all-to-all-start.1 = ((f32[8,1,512]{2,1,0:T(1,128)}), f32[8,1,512]{2,1,0:T(1,128)S(1)}, u32[]{:S(2)}, u32[]{:S(2)}) async-start(f32[8,1,512]{2,1,0:T(1,128)} %reshape.110), calls=%async_computation.1 | async-start | bytes 32768 | tf_op jit(solution)/shard_map/all_to_all | solution.py:94
  204.4 23.5 %all-to-all-start = ((f32[8,1,32768]{2,1,0:T(1,128)}), f32[8,1,32768]{2,1,0:T(1,128)S(1)}, u32[]{:S(2)}, u32[]{:S(2)}) async-start(f32[8,1,32768]{2,1,0:T(1,128)} %reshape.108), calls=%async_computation | async-start | bytes 2097152 | tf_op jit(solution)/shard_map/all_to_all | solution.py:96
  209.4 99.2 %reduce-scatter.4.cloned.1.call-start = ((), (), s32[]{:S(2)}) async-start(), calls=%async_computation.4 | async-start | bytes 688128
Sparse Core Ops, SparseCore 0:
  303.7 4.9 reduce-scatter.3
where the time goes:
time: 320 us; the launch traced here: 317 us
  matrix products  110 us (34%)
  blocking collectives  74.7 us (23%)
  local copies, waits for them, and re-layouts  51.6 us (16%)
  waiting for transfers between devices  27.9 us (9%)
  other arithmetic  24.3 us (8%)
  starting transfers between devices  13.9 us (4%)
  between operations  13.5 us (4%)
    psum x1, blocking collectives, local(): value_rows = lax.psum(value_slice, 'seq').astype(jnp.bfloat16)  38.2 us
    all_gather x1, blocking collectives, local(): q_latent = lax.all_gather(q_part, 'seq', axis=2, tiled=True)  36.4 us
    dot_general x16, matrix products, update(): jnp.einsum('bsh,shk->bhk', factor, slot_out, precision=peak_score)  28.3 us
    dot_general x16, matrix products, update(): jnp.einsum('sht,stk->shk', exponent.astype(jnp.bfloat16), latent_block, p...  24.3 us
    dot_general x16, matrix products, update(): jnp.einsum('shk,stk->sht', pick_latent, latent_block, preferred_element_t...  22 us
    all_to_all x1, waiting for transfers between devices, local(): lax.all_to_all(run_out, 'seq', split_axis=2, concat_axis=2, tiled=True)  16 us
    dynamic_slice x16, local copies, waits for them, and re-layouts, update(): lax.dynamic_slice_in_dim(rope_cache, start, 8, 0)  13.5 us
    unnamed x13, local copies, waits for them, and re-layouts  12 us
  transfers between devices with their start and end apart: 4, of which 4 were waited for; matrix products, arithmetic and copies ran while one was open for 3% of the time, Pallas kernels for 0%

commit v1 on v0

--- a/solution.py
+++ b/solution.py
@@ -93,7 +93,12 @@
     peers_max, peers_sum, peers_out = (
         lax.all_to_all(spread_max, "seq", split_axis=2, concat_axis=2, tiled=True),
         lax.all_to_all(spread_sum, "seq", split_axis=2, concat_axis=2, tiled=True),
-        lax.all_to_all(run_out, "seq", split_axis=2, concat_axis=2, tiled=True),
+        jnp.concatenate(
+            lax.all_to_all(
+                jnp.stack(jnp.split(run_out, lax.axis_size("seq"), axis=2)), "seq", 0, 0
+            ),
+            axis=2,
+        ),
     )
     top = jnp.max(peers_max, axis=2)
     rescale = jnp.exp(peers_max - top[:, :, None])

time: 320 us -> 354 us (1.11)
  matrix products: 110 us -> 141 us
  other arithmetic: 24.3 us -> 37.5 us
  local copies, waits for them, and re-layouts: 51.6 us -> 43.2 us
    add x16, other arithmetic: 0.36 us -> 21.4 us  [update(): run_sum * carry_scale]
    dot_general x16, matrix products: 5.57 us -> 22.2 us  [update(): jnp.einsum('bs,bhk->shk', owner_block, q_latent, preferred_element_type=j...]
    dot_general x16, matrix products: 3.62 us -> 18.3 us  [update(): jnp.einsum('bs,bhr->shr', owner_block, q_rope, preferred_element_type=jnp...]
    reshape x1 -> x0, local copies, waits for them, and re-layouts: 9.39 us -> none  [local(): grouped = peers_out.reshape(seq_count, heads, shards, share_width)]
    reduce_sum x1, other arithmetic: 9.67 us -> 1.94 us  [local(): shared_latent = jnp.sum(grouped * rescale[:, :, :, None], axis=2)]
    unnamed x13 -> x24, local copies, waits for them, and re-layouts: 12 us -> 17 us
  transfers between devices with their start and end apart: 4 -> 4, of which waited for: 4 -> 4; matrix products, arithmetic and copies ran while one was open for 3% -> 4% of each run, Pallas kernels for 0% -> 0%
where the time goes in v1:
time: 354 us; the launch traced here: 349 us
  matrix products  141 us (40%)
  blocking collectives  72.8 us (21%)
  local copies, waits for them, and re-layouts  43.2 us (12%)
  other arithmetic  37.5 us (11%)
  waiting for transfers between devices  24.8 us (7%)
  starting transfers between devices  14.8 us (4%)
  between operations  13.5 us (4%)
    psum x1, blocking collectives, local(): value_rows = lax.psum(value_slice, 'seq').astype(jnp.bfloat16)  38.2 us
    all_gather x1, blocking collectives, local(): q_latent = lax.all_gather(q_part, 'seq', axis=2, tiled=True)  34.6 us
    dot_general x16, matrix products, update(): jnp.einsum('bsh,shk->bhk', factor, slot_out, precision=peak_score)  28.3 us
    dot_general x16, matrix products, update(): jnp.einsum('sht,stk->shk', exponent.astype(jnp.bfloat16), latent_block, p...  24.3 us
    dot_general x16, matrix products, update(): jnp.einsum('bs,bhk->shk', owner_block, q_latent, preferred_element_type=j...  22.2 us
    dot_general x16, matrix products, update(): jnp.einsum('shk,stk->sht', pick_latent, latent_block, preferred_element_t...  22 us
    add x16, other arithmetic, update(): run_sum * carry_scale  21.4 us
    dot_general x16, matrix products, update(): jnp.einsum('bs,bhr->shr', owner_block, q_rope, preferred_element_type=jnp...  18.3 us
  transfers between devices with their start and end apart: 4, of which 4 were waited for; matrix products, arithmetic and copies ran while one was open for 4% of the time, Pallas kernels for 0%

profile of v1, /device:TPU:0, one launch (start us, length us, event | category | flops | bytes accessed | tf_op | source)
XLA Modules:
  0.0 349.3 jit_solution(11930661633004383327)
XLA Ops:
  10.1 1.9 fusion.41
  12.2 34.6 %all_gather.3 = bf16[8,64,512]{1,0,2:T(8,128)(2,1)S(1)} all-gather(bf16[8,64,64]{1,0,2:T(8,128)(2,1)S(1)} %copy.41), channel_id=1, replica_groups=mesh['groups'=2,'seq'=8,'mp'=2] {'seq'}, dimensions={2}, use_global_device_ids=true | all-gather | bytes 589824 | tf_op jit(solution)/shard_map/all_gather | solution.py:20
  46.8 2.0 copy.43
  49.5 182.4 %while.18 = (s32[]{:T(128)}, f32[8,64]{0,1:T(8,128)S(1)}, f32[8,64]{0,1:T(8,128)}, f32[8,64,512]{2,0,1:T(8,128)S(1)}, bf16[8,128]{1,0:T(8,128)(2,1)S(1)}, /*inde...) while((s32[]{:T(128)}, f32[8,64]{0,1:T(8,128)S(1)}, ...), condition=%wide.region_6.7_spmd.clone, body=%wide.region_2.6_spmd.clone.sunk | while | flops 102681152 | bytes 8060523 | solution.py:88
  55.0 1.5 fusion.91
  58.4 1.8 fusion.92
  69.9 1.8 fusion.92
  77.1 1.5 fusion.91
  81.3 1.8 fusion.92
  88.6 1.5 fusion.91
  92.8 1.8 fusion.92
  100.0 1.5 fusion.91
  104.2 1.8 fusion.92
  111.5 1.5 fusion.91
  115.7 1.8 fusion.92
  122.9 1.5 fusion.91
  127.1 1.8 fusion.92
  134.3 1.5 fusion.91
  138.6 1.8 fusion.92
  145.8 1.5 fusion.91
  150.0 1.8 fusion.92
  157.2 1.5 fusion.91
  161.5 1.8 fusion.92
  168.7 1.5 fusion.91
  172.9 1.8 fusion.92
  180.1 1.5 fusion.91
  184.4 1.8 fusion.92
  191.6 1.5 fusion.91
  195.8 1.8 fusion.92
  203.0 1.5 fusion.91
  207.3 1.8 fusion.92
  214.5 1.5 fusion.91
  218.7 1.8 fusion.92
  225.9 1.5 fusion.91
  230.2 1.8 fusion.92
  232.7 5.4 %all-to-all-start.1 = ((f32[8,1,512]{2,1,0:T(1,128)}), f32[8,1,512]{2,1,0:T(1,128)S(1)}, u32[]{:S(2)}, u32[]{:S(2)}) async-start(f32[8,1,512]{2,1,0:T(1,128)} %reshape.110), calls=%async_computation.1 | async-start | bytes 32768 | tf_op jit(solution)/shard_map/all_to_all | solution.py:94
  244.7 5.7 %all-to-all-start.2 = ((f32[8,1,512]{2,1,0:T(1,128)}), f32[8,1,512]{2,1,0:T(1,128)S(1)}, u32[]{:S(2)}, u32[]{:S(2)}) async-start(f32[8,1,512]{2,1,0:T(1,128)} %reshape.112), calls=%async_computation.2 | async-start | bytes 32768 | tf_op jit(solution)/shard_map/all_to_all | solution.py:95
  251.2 3.4 reshape.108
  254.6 2.5 all-to-all-done.2
  257.0 3.6 %all-to-all-start = ((f32[8,1,32768]{2,1,0:T(1,128)}), f32[8,1,32768]{2,1,0:T(1,128)S(1)}, u32[]{:S(2)}, u32[]{:S(2)}) async-start(f32[8,1,32768]{2,1,0:T(1,128)} %reshape.108), calls=%async_computation | async-start | bytes 2097152 | tf_op jit(solution)/shard_map/all_to_all | solution.py:97
  263.1 16.7 %all-to-all-done = f32[8,1,32768]{2,1,0:T(1,128)S(1)} async-done(((f32[8,1,32768]{2,1,0:T(1,128)}), f32[8,1,32768]{2,1,0:T(1,128)S(1)}, u32[]{:S(2)}, u32[]{:S(2)}) %all-to-all-start) | async-done | bytes 1048608 | tf_op jit(solution)/shard_map/all_to_all | solution.py:97
  279.9 3.1 reduce.2
  283.0 2.2 reshape.109
  285.2 1.9 fusion.40
  287.6 38.2 %all-reduce.1 = bf16[8,64,128]{2,0,1:T(8,128)(2,1)S(1)} all-reduce(f32[8,64,128]{2,0,1:T(8,128)S(1)} %convolution_bitcast_fusion.2), channel_id=1, replica_groups=mesh['groups'=2,'seq'=8,'mp'=2] {'seq'}, use_global_device_ids=true, to_apply=%region_10.11 | all-reduce | flops 65536 | bytes 393216 | tf_op jit(solution)/shard_map/psum | solution.py:112
  325.8 9.8 %convolution_bitcast_fusion.1 = f32[896,8]{1,0:T(8,128)} fusion(bf16[8192,896]{1,0:T(8,128)(2,1)} %param.17, bf16[8,64,128]{2,0,1:T(8,128)(2,1)S(1)} %all-reduce.1), kind=kOutput, calls=%fused_computation.55 | convolution fusion | flops 117440512 | bytes 14839808
  335.6 5.2 %reduce-scatter.4.cloned.1.call-done = f32[448,8]{1,0:T(8,128)} async-done(((f32[896,8]{1,0:T(8,128)}), f32[448,8]{1,0:T(8,128)}) %reduce-scatter.4.cloned.1.call-update) | async-done | bytes 14352
  340.8 1.6 copy.53
  (430 shorter events, 145.0 us)
Async XLA Ops:
  6.5 280.6 %copy-start = (bf16[64,64,128]{2,1,0:T(8,128)(2,1)S(1)}, bf16[64,64,128]{2,1,0:T(8,128)(2,1)}, u32[]{:S(2)}) copy-start(bf16[64,64,128]{2,1,0:T(8,128)(2,1)} %param.16) | copy-start | bytes 3145732
  10.1 38.7 %copy-start.2 = (bf16[8,64,64]{2,1,0:T(8,128)(2,1)S(1)}, bf16[8,64,64]{2,1,0:T(8,128)(2,1)}, u32[]{:S(2)}) copy-start(bf16[8,64,64]{2,1,0:T(8,128)(2,1)} %param.14) | copy-start | bytes 196612
  49.5 5.0 %copy-start.3 = (s32[128]{0:T(128)}, s32[128]{0:T(128)S(1)}, u32[]{:S(2)}) copy-start(s32[128]{0:T(128)S(1)} %get-tuple-element.382) | copy-start | bytes 1540 | tf_op jit(solution)/shard_map/while
  57.1 3.1 copy-start.4
  60.2 5.0 %copy-start.3 = (s32[128]{0:T(128)}, s32[128]{0:T(128)S(1)}, u32[]{:S(2)}) copy-start(s32[128]{0:T(128)S(1)} %get-tuple-element.382) | copy-start | bytes 1540 | tf_op jit(solution)/shard_map/while
  67.8 3.9 %copy-start.4 = (s32[128]{0:T(128)S(1)}, s32[128]{0:T(128)}, u32[]{:S(2)}) copy-start(s32[128]{0:T(128)} %copy-done.3) | copy-start | bytes 1540 | tf_op jit(solution)/shard_map/while
  71.7 5.0 %copy-start.3 = (s32[128]{0:T(128)}, s32[128]{0:T(128)S(1)}, u32[]{:S(2)}) copy-start(s32[128]{0:T(128)S(1)} %get-tuple-element.382) | copy-start | bytes 1540 | tf_op jit(solution)/shard_map/while
  79.2 3.9 %copy-start.4 = (s32[128]{0:T(128)S(1)}, s32[128]{0:T(128)}, u32[]{:S(2)}) copy-start(s32[128]{0:T(128)} %copy-done.3) | copy-start | bytes 1540 | tf_op jit(solution)/shard_map/while
  83.1 5.0 %copy-start.3 = (s32[128]{0:T(128)}, s32[128]{0:T(128)S(1)}, u32[]{:S(2)}) copy-start(s32[128]{0:T(128)S(1)} %get-tuple-element.382) | copy-start | bytes 1540 | tf_op jit(solution)/shard_map/while
  90.7 3.9 %copy-start.4 = (s32[128]{0:T(128)S(1)}, s32[128]{0:T(128)}, u32[]{:S(2)}) copy-start(s32[128]{0:T(128)} %copy-done.3) | copy-start | bytes 1540 | tf_op jit(solution)/shard_map/while
  94.6 5.0 %copy-start.3 = (s32[128]{0:T(128)}, s32[128]{0:T(128)S(1)}, u32[]{:S(2)}) copy-start(s32[128]{0:T(128)S(1)} %get-tuple-element.382) | copy-start | bytes 1540 | tf_op jit(solution)/shard_map/while
  102.1 3.9 %copy-start.4 = (s32[128]{0:T(128)S(1)}, s32[128]{0:T(128)}, u32[]{:S(2)}) copy-start(s32[128]{0:T(128)} %copy-done.3) | copy-start | bytes 1540 | tf_op jit(solution)/shard_map/while
  106.0 5.0 %copy-start.3 = (s32[128]{0:T(128)}, s32[128]{0:T(128)S(1)}, u32[]{:S(2)}) copy-start(s32[128]{0:T(128)S(1)} %get-tuple-element.382) | copy-start | bytes 1540 | tf_op jit(solution)/shard_map/while
  113.6 3.9 %copy-start.4 = (s32[128]{0:T(128)S(1)}, s32[128]{0:T(128)}, u32[]{:S(2)}) copy-start(s32[128]{0:T(128)} %copy-done.3) | copy-start | bytes 1540 | tf_op jit(solution)/shard_map/while
  117.5 5.0 %copy-start.3 = (s32[128]{0:T(128)}, s32[128]{0:T(128)S(1)}, u32[]{:S(2)}) copy-start(s32[128]{0:T(128)S(1)} %get-tuple-element.382) | copy-start | bytes 1540 | tf_op jit(solution)/shard_map/while
  125.0 3.9 %copy-start.4 = (s32[128]{0:T(128)S(1)}, s32[128]{0:T(128)}, u32[]{:S(2)}) copy-start(s32[128]{0:T(128)} %copy-done.3) | copy-start | bytes 1540 | tf_op jit(solution)/shard_map/while
  128.9 5.0 %copy-start.3 = (s32[128]{0:T(128)}, s32[128]{0:T(128)S(1)}, u32[]{:S(2)}) copy-start(s32[128]{0:T(128)S(1)} %get-tuple-element.382) | copy-start | bytes 1540 | tf_op jit(solution)/shard_map/while
  136.5 3.9 %copy-start.4 = (s32[128]{0:T(128)S(1)}, s32[128]{0:T(128)}, u32[]{:S(2)}) copy-start(s32[128]{0:T(128)} %copy-done.3) | copy-start | bytes 1540 | tf_op jit(solution)/shard_map/while
  140.4 5.0 %copy-start.3 = (s32[128]{0:T(128)}, s32[128]{0:T(128)S(1)}, u32[]{:S(2)}) copy-start(s32[128]{0:T(128)S(1)} %get-tuple-element.382) | copy-start | bytes 1540 | tf_op jit(solution)/shard_map/while
  147.9 3.9 %copy-start.4 = (s32[128]{0:T(128)S(1)}, s32[128]{0:T(128)}, u32[]{:S(2)}) copy-start(s32[128]{0:T(128)} %copy-done.3) | copy-start | bytes 1540 | tf_op jit(solution)/shard_map/while
  151.8 5.0 %copy-start.3 = (s32[128]{0:T(128)}, s32[128]{0:T(128)S(1)}, u32[]{:S(2)}) copy-start(s32[128]{0:T(128)S(1)} %get-tuple-element.382) | copy-start | bytes 1540 | tf_op jit(solution)/shard_map/while
  159.4 3.9 %copy-start.4 = (s32[128]{0:T(128)S(1)}, s32[128]{0:T(128)}, u32[]{:S(2)}) copy-start(s32[128]{0:T(128)} %copy-done.3) | copy-start | bytes 1540 | tf_op jit(solution)/shard_map/while
  163.3 5.0 %copy-start.3 = (s32[128]{0:T(128)}, s32[128]{0:T(128)S(1)}, u32[]{:S(2)}) copy-start(s32[128]{0:T(128)S(1)} %get-tuple-element.382) | copy-start | bytes 1540 | tf_op jit(solution)/shard_map/while
  170.8 3.9 %copy-start.4 = (s32[128]{0:T(128)S(1)}, s32[128]{0:T(128)}, u32[]{:S(2)}) copy-start(s32[128]{0:T(128)} %copy-done.3) | copy-start | bytes 1540 | tf_op jit(solution)/shard_map/while
  174.7 5.0 %copy-start.3 = (s32[128]{0:T(128)}, s32[128]{0:T(128)S(1)}, u32[]{:S(2)}) copy-start(s32[128]{0:T(128)S(1)} %get-tuple-element.382) | copy-start | bytes 1540 | tf_op jit(solution)/shard_map/while
  182.3 3.9 %copy-start.4 = (s32[128]{0:T(128)S(1)}, s32[128]{0:T(128)}, u32[]{:S(2)}) copy-start(s32[128]{0:T(128)} %copy-done.3) | copy-start | bytes 1540 | tf_op jit(solution)/shard_map/while
  186.2 5.0 %copy-start.3 = (s32[128]{0:T(128)}, s32[128]{0:T(128)S(1)}, u32[]{:S(2)}) copy-start(s32[128]{0:T(128)S(1)} %get-tuple-element.382) | copy-start | bytes 1540 | tf_op jit(solution)/shard_map/while
  193.7 3.9 %copy-start.4 = (s32[128]{0:T(128)S(1)}, s32[128]{0:T(128)}, u32[]{:S(2)}) copy-start(s32[128]{0:T(128)} %copy-done.3) | copy-start | bytes 1540 | tf_op jit(solution)/shard_map/while
  197.6 5.0 %copy-start.3 = (s32[128]{0:T(128)}, s32[128]{0:T(128)S(1)}, u32[]{:S(2)}) copy-start(s32[128]{0:T(128)S(1)} %get-tuple-element.382) | copy-start | bytes 1540 | tf_op jit(solution)/shard_map/while
  205.1 3.9 %copy-start.4 = (s32[128]{0:T(128)S(1)}, s32[128]{0:T(128)}, u32[]{:S(2)}) copy-start(s32[128]{0:T(128)} %copy-done.3) | copy-start | bytes 1540 | tf_op jit(solution)/shard_map/while
  209.1 5.0 %copy-start.3 = (s32[128]{0:T(128)}, s32[128]{0:T(128)S(1)}, u32[]{:S(2)}) copy-start(s32[128]{0:T(128)S(1)} %get-tuple-element.382) | copy-start | bytes 1540 | tf_op jit(solution)/shard_map/while
  216.6 3.9 %copy-start.4 = (s32[128]{0:T(128)S(1)}, s32[128]{0:T(128)}, u32[]{:S(2)}) copy-start(s32[128]{0:T(128)} %copy-done.3) | copy-start | bytes 1540 | tf_op jit(solution)/shard_map/while
  220.5 5.0 %copy-start.3 = (s32[128]{0:T(128)}, s32[128]{0:T(128)S(1)}, u32[]{:S(2)}) copy-start(s32[128]{0:T(128)S(1)} %get-tuple-element.382) | copy-start | bytes 1540 | tf_op jit(solution)/shard_map/while
  228.0 3.9 %copy-start.4 = (s32[128]{0:T(128)S(1)}, s32[128]{0:T(128)}, u32[]{:S(2)}) copy-start(s32[128]{0:T(128)} %copy-done.3) | copy-start | bytes 1540 | tf_op jit(solution)/shard_map/while
  232.0 11.6 %copy-start.1 = (f32[8,64]{0,1:T(8,128)S(1)}, f32[8,64]{0,1:T(8,128)}, u32[]{:S(2)}) copy-start(f32[8,64]{0,1:T(8,128)} %get-tuple-element.178) | copy-start | bytes 6148
  232.7 11.9 %all-to-all-start.1 = ((f32[8,1,512]{2,1,0:T(1,128)}), f32[8,1,512]{2,1,0:T(1,128)S(1)}, u32[]{:S(2)}, u32[]{:S(2)}) async-start(f32[8,1,512]{2,1,0:T(1,128)} %reshape.110), calls=%async_computation.1 | async-start | bytes 32768 | tf_op jit(solution)/shard_map/all_to_all | solution.py:94
  244.7 12.4 %all-to-all-start.2 = ((f32[8,1,512]{2,1,0:T(1,128)}), f32[8,1,512]{2,1,0:T(1,128)S(1)}, u32[]{:S(2)}, u32[]{:S(2)}) async-start(f32[8,1,512]{2,1,0:T(1,128)} %reshape.112), calls=%async_computation.2 | async-start | bytes 32768 | tf_op jit(solution)/shard_map/all_to_all | solution.py:95
  257.0 22.8 %all-to-all-start = ((f32[8,1,32768]{2,1,0:T(1,128)}), f32[8,1,32768]{2,1,0:T(1,128)S(1)}, u32[]{:S(2)}, u32[]{:S(2)}) async-start(f32[8,1,32768]{2,1,0:T(1,128)} %reshape.108), calls=%async_computation | async-start | bytes 2097152 | tf_op jit(solution)/shard_map/all_to_all | solution.py:97
  260.6 80.2 %reduce-scatter.4.cloned.1.call-start = ((), (), s32[]{:S(2)}) async-start(), calls=%async_computation.4 | async-start | bytes 688128
Sparse Core Ops, SparseCore 0:
  335.7 5.0 reduce-scatter.3
